TPU v7x, 256 devices: a whole 4x4x8 slice. The times are simulated.
256 devices in a mesh: unit: 2 (over core), block: 32 (over z, y), lane: 4 (over x).
Axes of the slice: x: 4, y: 4, z: 8, core: 2. Of those that a mesh axis runs over, the one named last changes fastest.
Arguments:
- image_rows: bfloat16 [16384, 512], P(('unit', 'block', 'lane')), parts along dimension 0, may hold values from -6 to 6, as said below
- text_rows: bfloat16 [16384, 512], P(('unit', 'block', 'lane')), parts along dimension 0, may hold values from -6 to 6, as said below
Outputs:
- image_loss: float32 [16384], P(('unit', 'block', 'lane')), parts along dimension 0
- text_loss: float32 [16384], P(('unit', 'block', 'lane')), parts along dimension 0
- image_grad: float32 [16384, 512], P(('unit', 'block', 'lane')), parts along dimension 0
- text_grad: float32 [16384, 512], P(('unit', 'block', 'lane')), parts along dimension 0
There are 2 independent parts, one for each index of `unit`. A program takes and returns all parts, laid end to end along the dimension named above; each array names one. Nothing has to cross between parts.
Inputs may be any that keep to these rules, and one draw needn't show every extreme that they name: image_rows holds numbers from -6 to 6. text_rows holds numbers from -6 to 6.
All inputs are finite; a program needn't handle non-finite values.
Results may differ from a plain program's by a relative error of at most 0.0035.
Values may be sent and summed in bfloat16 or wider, within the bound.
A program may use at most 64 MiB of HBM per device.

v0:
```python
import functools

import jax
import jax.numpy as jnp
from jax import lax
from jax.experimental import pallas as pl
from jax.experimental.pallas import tpu as pltpu
from jax.sharding import PartitionSpec as P

NT = (((1,), (1,)), ((), ()))
TN = (((0,), (0,)), ((), ()))
LOG2E = 1.4426950408889634
F32, BF16 = jnp.float32, jnp.bfloat16
PIECES = 2
RECV_SEMS = (12, 22)
BACK_ORDER = [(1, 12, 16), (0, 4, 8), (1, 8, 12), (0, 0, 4), (1, 4, 8), (1, 0, 4)]
IMAGE_GROUPS, TEXT_GROUPS = (4, 4), (4, 4, 8)

PLANS = [
    (
        (
            [
                ((4,), 1, (2,), 10.8), ((2,), 0, (1,), 6.9), ((3,), 0, (1,), 8.2), ((3,), 1, (1,), 9.5),
                ((6,), 0, (0,), 5.8), ((2,), 1, (0,), 5.8), ((7,), 1, (0,), 3.4), ((7,), 0, (0,), 4.1),
                ((6,), 1, (7,), 6.9), ((1,), 0, (0,), 3.4), ((5,), 0, (7,), 9.5), ((4,), 0, (6,), 10.8),
                ((1,), 1, (0,), 4.1), ((5,), 1, (7,), 8.2),
            ],
            [
                ((5,), 0, (6,), 4.3), ((1,), 0, (0,), 6.9), ((2,), 1, (0,), 8.8), ((6,), 0, (0,), 8.8),
                ((1,), 1, (0,), 7.5), ((3,), 1, (2,), 4.3), ((7,), 1, (0,), 6.9), ((5,), 1, (6,), 4.9),
                ((7,), 0, (0,), 7.5), ((6,), 1, (0,), 10.4), ((3,), 0, (2,), 4.9), ((4,), 0, (2,), 6.2),
                ((2,), 0, (0,), 10.4), ((4,), 1, (6,), 6.2),
            ],
        ),
        (
            [
                ((3, 2), 0, (3, 3), 10.8), ((2, 0), 1, (3, 0), 7.0), ((2, 3), 0, (1, 3), 10.3), ((1, 0), 0, (0, 0), 3.4),
                ((1, 1), 1, (0, 1), 7.0), ((0, 2), 0, (0, 3), 6.9), ((3, 0), 1, (0, 0), 3.4), ((0, 1), 1, (0, 0), 3.4),
                ((2, 2), 0, (1, 3), 10.9), ((0, 3), 0, (0, 0), 3.4), ((3, 1), 1, (0, 0), 5.7), ((1, 0), 1, (0, 0), 4.1),
                ((1, 3), 0, (0, 0), 5.7), ((3, 3), 1, (3, 0), 7.6), ((1, 1), 0, (0, 0), 6.4), ((3, 0), 0, (0, 0), 4.1),
                ((2, 2), 1, (3, 1), 10.1), ((1, 3), 1, (0, 3), 8.3), ((2, 1), 0, (3, 0), 8.8), ((2, 0), 0, (1, 0), 7.7),
                ((2, 1), 1, (3, 0), 7.7), ((0, 1), 0, (0, 0), 4.1), ((0, 2), 1, (0, 1), 7.6), ((3, 1), 0, (3, 0), 8.9),
                ((1, 2), 0, (1, 3), 10.2), ((3, 3), 0, (0, 0), 6.4), ((0, 3), 1, (0, 0), 4.1), ((1, 2), 1, (0, 3), 9.0),
                ((3, 2), 1, (3, 1), 10.2), ((2, 3), 1, (1, 0), 9.6),
            ],
            [
                ((3, 0), 0, (0, 0), 7.2), ((1, 0), 1, (0, 0), 7.8), ((2, 1), 1, (3, 1), 5.2), ((0, 3), 0, (0, 0), 10.7),
                ((2, 3), 1, (1, 3), 3.9), ((3, 1), 0, (0, 1), 5.9), ((2, 2), 1, (1, 3), 4.6), ((1, 1), 1, (0, 0), 8.6),
                ((3, 1), 1, (0, 0), 9.3), ((1, 2), 0, (1, 3), 4.6), ((2, 0), 0, (1, 0), 6.5), ((1, 3), 0, (0, 0), 9.9),
                ((0, 2), 1, (0, 1), 6.5), ((2, 3), 0, (3, 3), 3.9), ((3, 2), 0, (0, 1), 4.6), ((3, 0), 1, (0, 0), 10.0),
                ((1, 1), 0, (1, 0), 7.2), ((0, 3), 1, (0, 0), 5.9), ((2, 2), 0, (1, 3), 5.8), ((1, 2), 1, (1, 1), 4.6),
                ((3, 2), 1, (3, 1), 5.2), ((0, 1), 0, (0, 0), 9.4), ((3, 3), 1, (3, 0), 6.5), ((1, 0), 0, (0, 0), 10.7),
                ((2, 0), 1, (3, 0), 6.5), ((1, 3), 1, (0, 0), 9.3), ((0, 2), 0, (0, 3), 7.2), ((3, 3), 0, (0, 0), 8.4),
                ((2, 1), 0, (1, 0), 7.1), ((0, 1), 1, (0, 0), 10.0),
            ],
        ),
    ),
    (
        (
            [
                ((5,), 1, (6,), 7.1), ((6,), 1, (0,), 4.5), ((5,), 0, (7,), 5.8), ((7,), 0, (0,), 2.4),
                ((4,), 0, (5,), 8.3), ((6,), 0, (7,), 6.4), ((1,), 1, (0,), 2.4), ((2,), 0, (0,), 4.5),
                ((7,), 1, (0,), 3.1), ((3,), 1, (1,), 5.8), ((2,), 1, (1,), 6.4), ((3,), 0, (2,), 7.1),
                ((1,), 0, (0,), 3.1), ((4,), 1, (3,), 8.3),
            ],
            [
                ((7,), 0, (0,), 4.6), ((1,), 1, (0,), 4.6), ((2,), 0, (0,), 9.0), ((3,), 0, (2,), 5.9),
                ((4,), 0, (3,), 3.3), ((3,), 1, (2,), 3.9), ((1,), 0, (0,), 5.2), ((5,), 1, (6,), 5.9),
                ((2,), 1, (0,), 7.2), ((6,), 1, (0,), 9.0), ((4,), 1, (5,), 3.3), ((6,), 0, (0,), 7.2),
                ((5,), 0, (6,), 3.9), ((7,), 1, (0,), 5.2),
            ],
        ),
        (
            [
                ((1, 2), 1, (1, 1), 8.0), ((1, 1), 1, (0, 1), 5.1), ((2, 2), 1, (2, 3), 8.6), ((2, 3), 1, (1, 0), 6.1),
                ((1, 0), 0, (0, 0), 2.4), ((3, 0), 1, (0, 0), 2.4), ((3, 1), 1, (0, 0), 4.4), ((3, 0), 0, (0, 0), 3.1),
                ((0, 3), 0, (0, 0), 2.4), ((1, 1), 0, (1, 0), 4.9), ((0, 2), 1, (0, 3), 6.2), ((1, 2), 0, (1, 1), 7.4),
                ((3, 3), 0, (0, 3), 5.1), ((0, 1), 1, (0, 0), 2.4), ((3, 3), 1, (3, 0), 4.9), ((2, 1), 1, (3, 1), 7.0),
                ((3, 2), 1, (3, 3), 7.5), ((2, 0), 0, (3, 0), 6.4), ((2, 1), 0, (1, 1), 8.1), ((1, 3), 0, (0, 0), 4.4),
                ((2, 3), 0, (3, 3), 7.7), ((3, 1), 0, (3, 0), 5.6), ((1, 3), 1, (0, 3), 6.8), ((2, 2), 0, (1, 3), 7.5),
                ((2, 0), 1, (3, 0), 5.7), ((0, 3), 1, (0, 0), 3.1), ((1, 0), 1, (0, 0), 3.1), ((0, 1), 0, (0, 0), 3.1),
                ((0, 2), 0, (0, 1), 6.2), ((3, 2), 0, (0, 2), 8.7),
            ],
            [
                ((0, 3), 0, (0, 0), 6.8), ((2, 2), 1, (1, 2), 2.9), ((0, 2), 0, (0, 1), 4.9), ((1, 1), 0, (0, 1), 4.9),
                ((1, 1), 1, (0, 1), 5.5), ((1, 3), 1, (1, 0), 3.6), ((2, 0), 1, (3, 0), 4.9), ((2, 0), 0, (1, 0), 3.6),
                ((1, 3), 0, (0, 0), 8.1), ((3, 2), 1, (3, 1), 2.9), ((3, 1), 0, (0, 0), 7.3), ((3, 3), 0, (3, 0), 5.5),
                ((2, 1), 0, (3, 1), 2.9), ((0, 1), 0, (0, 0), 7.4), ((0, 3), 1, (0, 0), 8.1), ((0, 1), 1, (0, 0), 8.7),
                ((0, 2), 1, (0, 3), 4.2), ((2, 3), 0, (1, 3), 4.2), ((3, 1), 1, (0, 1), 6.2), ((1, 0), 0, (0, 0), 6.8),
                ((2, 1), 1, (3, 1), 3.6), ((2, 2), 0, (3, 1), 4.2), ((1, 0), 1, (0, 0), 7.5), ((1, 2), 0, (1, 3), 2.9),
                ((1, 2), 1, (0, 1), 6.2), ((3, 2), 0, (3, 1), 4.2), ((3, 3), 1, (3, 0), 6.2), ((2, 3), 1, (3, 0), 5.5),
                ((3, 0), 0, (0, 0), 8.0), ((3, 0), 1, (0, 0), 8.7),
            ],
        ),
    ),
]


def rectangles(cells):
    found = []
    for h in sorted({h for h, _ in cells}):
        runs = []
        for g in sorted(g for k, g in cells if k == h):
            if runs and runs[-1][-1] == g - 1:
                runs[-1].append(g)
            else:
                runs.append([g])
        for run in runs:
            match = [hs for hs, gs in found if gs == run and hs[-1] == h - 1]
            if match:
                match[0].append(h)
            else:
                found.append(([h], run))
    return found


class Group:
    def __init__(self, route, sizes, here, device):
        self.sizes, self.here, self.device_of = sizes, here, device
        self.home = (0,) * len(sizes)
        when = {self.home: 0.0}
        for o, _, _, t in route:
            when[self.neg(o)] = max(t, when.get(self.neg(o), 0.0))
        self.slots = sorted(when, key=when.get)

    def sub(self, a, b):
        return tuple((i - j) % n for i, j, n in zip(a, b, self.sizes))

    def neg(self, a):
        return tuple(-i % n for i, n in zip(a, self.sizes))

    def at(self, a):
        return [lax.rem(h + i, n) if i else h for h, i, n in zip(self.here, a, self.sizes)]

    def device(self, a):
        return self.device_of(*self.at(a))

    def index(self, a):
        index = 0
        for i, n in zip(self.at(a), self.sizes):
            index = index * n + i
        return index


def unit_rows(values):
    wide = values.astype(F32)
    scale = lax.rsqrt(jnp.sum(wide * wide, axis=-1, keepdims=True) + 1e-06)
    return (wide * scale).astype(BF16)


def upright(row):
    return jnp.transpose(jnp.broadcast_to(row, (8, row.shape[1])))[:, :1]


class Side:
    def __init__(self, group, group_of, routes, rows, data, sums, mine, own, out, inbox, sems):
        self.g, self.rows, self.data, self.sums, self.mine = group, rows, data, sums, mine
        self.out_route, self.back_route = routes
        self.own, self.out, self.inbox = own, out, inbox
        self.send, self.recv, self.sum_recv = sems
        self.pos = {slot: k for k, slot in enumerate(group.slots)}
        self.home = group.home
        self.landed = set()
        g = group

        def remote(send, src, dst, recv, offset):
            return pltpu.make_async_remote_copy(
                src_ref=src, dst_ref=dst, send_sem=self.send.at[send], recv_sem=recv, device_id=g.device(offset)
            )

        self.out_pools, self.back_pools = self.pools(group_of)
        assert max(len(self.out_pools), len(self.back_pools)) <= self.recv.shape[0]
        out_pool, back_pool = ({k: n for n, ks in enumerate(pools) for k in ks} for pools in (self.out_pools, self.back_pools))
        self.gather = [
            remote(
                0, data.at[self.piece(g.neg(r), p)], data.at[self.piece(g.neg(o), p)],
                self.recv.at[out_pool[k]], g.sub(o, r),
            )
            for k, (o, p, r, _) in enumerate(self.out_route)
        ]
        self.exchange = [
            remote(1, mine, sums.at[k], self.sum_recv.at[0], o) for k, o in enumerate(reversed(g.slots[1:]))
        ]
        self.reduce = [
            remote(0, out.at[self.piece(g.neg(o), p)], inbox.at[k], self.recv.at[back_pool[k]], g.sub(r, o))
            for k, (o, p, r, _) in enumerate(self.back_route)
        ]

    def pools(self, group_of):
        out, back = {}, {}
        for k, (o, p, _, _) in enumerate(self.out_route):
            out.setdefault(("at", k) if self.onward(o, p) else ("of", group_of[self.pos[self.g.neg(o)]]), []).append(k)
        for k, (_, p, r, _) in enumerate(self.back_route):
            if r != self.home:
                back.setdefault((r, p), []).append(k)
        home = [k for _, k in sorted(self.home_parts())]
        while home:
            count = min(4, max(1, len(home) // 2))
            back[home[0]], home = home[:count], home[count:]
        return list(out.values()), list(back.values())

    def wait_pool(self, pools, n):
        amount = self.inbox.at[pl.ds(0, len(pools[n]))]
        pltpu.make_async_copy(amount, amount, self.recv.at[n]).wait()

    def hops(self, offset):
        return sum(min(i, n - i) for i, n in zip(offset, self.g.sizes))

    def next_to(self):
        return [o for o in self.g.slots if self.hops(o) == 1]

    def piece(self, slot, p):
        size = self.rows // PIECES
        return pl.ds(self.pos[slot] * self.rows + p * size, size)

    def onward(self, o, p):
        return [k for k, (_, q, r, _) in enumerate(self.out_route) if r == o and q == p]

    def inward(self, o, p):
        parts = [(t, k) for k, (_, q, r, t) in enumerate(self.back_route) if r == o and q == p]
        return [k for _, k in sorted(parts)]

    def start_gather(self, hops):
        for k, (o, _, r, _) in enumerate(self.out_route):
            if r == self.home and self.hops(o) == hops:
                self.gather[k].start()

    def arrive(self, k):
        o, p, _, _ = self.out_route[k]
        pool = [n for n, ks in enumerate(self.out_pools) if k in ks][0]
        self.landed.add(k)
        if not self.landed.issuperset(self.out_pools[pool]):
            return
        self.wait_pool(self.out_pools, pool)
        for j in self.onward(o, p):
            assert self.hops(self.g.sub(self.out_route[j][0], o)) <= 2
            self.gather[j].start()

    def keep_sum(self, position, row):
        slot = self.g.slots[position]
        self.mine[pl.ds(self.g.index(slot), 1), 0 : self.rows] = row

    def start_sums(self):
        for copy in self.exchange:
            copy.start()

    def total(self):
        pltpu.make_async_copy(self.sums, self.sums, self.sum_recv.at[0]).wait()
        total = self.mine[...]
        for k in range(len(self.exchange)):
            total = total + self.sums[k]
        return total

    def send_ready(self, slots):
        for k, (o, p, _, _) in enumerate(self.back_route):
            if self.g.neg(o) in slots and not self.inward(o, p):
                self.reduce[k].start()

    def stops(self):
        parts = [(self.inward(o, p), k) for k, (o, p, _, _) in enumerate(self.back_route)]
        return [(self.back_route[inward[-1]][3], k) for inward, k in parts if inward]

    def pass_on(self, k):
        o, p, _, _ = self.back_route[k]
        where = self.piece(self.g.neg(o), p)
        total = self.own[where, :]
        parts = self.inward(o, p)
        self.wait_pool(self.back_pools, [n for n, ks in enumerate(self.back_pools) if parts[0] in ks][0])
        for j in parts:
            total = total + self.inbox[j].astype(F32)
        self.out[where, :] = total.astype(BF16)
        self.reduce[k].start()

    def home_parts(self):
        return [(t, k) for k, (_, _, r, t) in enumerate(self.back_route) if r == self.home]

    def home_pools(self):
        when = dict((k, t) for t, k in self.home_parts())
        return [(max(when[k] for k in ks), n) for n, ks in enumerate(self.back_pools) if ks[0] in when]

    def add_home(self, n, grad):
        size = self.rows // PIECES
        self.wait_pool(self.back_pools, n)
        for p in range(PIECES):
            parts = [k for k in self.back_pools[n] if self.back_route[k][1] == p]
            if parts:
                here = slice(p * size, (p + 1) * size)
                grad[here, :] = sum((self.inbox[k].astype(F32) for k in parts), grad[here, :])

    def wait_sends(self, n):
        amount = (self.inbox, self.sums)[n]
        pltpu.make_async_copy(amount, amount, self.send.at[n]).wait()


def kernel(
    side,
    image_hbm, text_hbm,
    image_loss, text_loss, image_grad, text_grad,
    image_raw, text_raw, images, texts, power, pull,
    row_mine, row_in, col_mine, col_in, row_tot, col_tot, row_all, col_all,
    image_own, text_own, image_out, text_out, image_box, text_box,
    around, *sems,
):
    lane, block, unit = lax.axis_index("lane"), lax.axis_index("block"), lax.axis_index("unit")
    z, y = block // side, lax.rem(block, side)
    rows = image_raw.shape[0]
    image_count = row_mine.shape[0]
    sizes = (IMAGE_GROUPS, TEXT_GROUPS)
    first = [[sum(s[:g]) for g in range(len(s) + 1)] for s in sizes]
    group_of = [[g for g, n in enumerate(s) for _ in range(n)] for s in sizes]

    loads = [
        pltpu.make_async_copy(image_hbm, image_raw, sems[0].at[0]),
        pltpu.make_async_copy(text_hbm, text_raw, sems[3].at[0]),
    ]
    for load in loads:
        load.start()
    barrier = pltpu.get_barrier_semaphore()

    def sides(plan):
        line = Group(plan[0][0], (image_count,), (z,), lambda k: {"block": k * side + y})
        plane = Group(plan[1][0], (side, side), (y, lane), lambda k, j: {"block": z * side + k, "lane": j})
        return (
            Side(line, group_of[0], plan[0], rows, images, row_in, row_mine, image_own, image_out, image_box, sems[:3]),
            Side(plane, group_of[1], plan[1], rows, texts, col_in, col_mine, text_own, text_out, text_box, sems[3:]),
        )

    def some(s, gs):
        start, end = first[s][gs[0]] * rows, first[s][gs[-1] + 1] * rows
        return pl.ds(start, end - start)

    def run(plan):
        image, text = sides(plan)
        for part in (image, text):
            for o in part.next_to():
                pl.semaphore_signal(barrier, inc=1, device_id=part.g.device(o))
        with jax.named_scope("load"):
            loads[1].wait()
            texts[0:rows, :] = unit_rows(text_raw[...])
            loads[0].wait()
            images[0:rows, :] = unit_rows(image_raw[...])
        with jax.named_scope("barrier"):
            pl.semaphore_wait(barrier, len(image.next_to()) + len(text.next_to()))
        for part in (image, text):
            for o in part.next_to():
                pl.semaphore_signal(around, inc=1, device_id=part.g.device(o))
        text.start_gather(1)
        image.start_gather(1)

        pair = 12.0 * lax.dot_general(images[0:rows, :], texts[0:rows, :], NT, preferred_element_type=F32)
        eye = lax.broadcasted_iota(jnp.int32, (rows, rows), 0) == lax.broadcasted_iota(jnp.int32, (rows, rows), 1)
        matched = jnp.sum(jnp.where(eye, pair, 0.0), axis=0, keepdims=True)

        with jax.named_scope("around"):
            pl.semaphore_wait(around, len(image.next_to()) + len(text.next_to()))
        text.start_gather(2)
        image.start_gather(2)

        row_sums, col_sums = [0.0] * len(IMAGE_GROUPS), [0.0] * len(TEXT_GROUPS)

        def powers(hs, gs):
            here, there = some(0, hs), some(1, gs)
            logit = lax.dot_general(images[here, :], texts[there, :], NT, preferred_element_type=F32)
            p = jnp.exp2((12.0 * LOG2E) * logit)
            power[here, there] = p
            lanes = sum(p[:, k : k + 128] for k in range(0, p.shape[1], 128))
            for s, groups, sums in ((0, hs, row_sums), (1, gs, col_sums)):
                start = 0
                for g in groups:
                    end = start + sizes[s][g] * rows
                    sums[g] += jnp.sum(p[:, start:end], axis=0, keepdims=True) if s else lanes[start:end]
                    start = end

        waits = sorted(
            (t, s, k) for s, part in enumerate((image, text)) for k, (_, _, _, t) in enumerate(part.out_route)
        )
        missing = {(s, g): set() for s in (0, 1) for g in range(len(sizes[s]))}
        for s, part in enumerate((image, text)):
            for k, (o, _, _, _) in enumerate(part.out_route):
                missing[(s, group_of[s][part.pos[part.g.neg(o)]])].add(k)
        todo = {(h, g) for h in range(len(IMAGE_GROUPS)) for g in range(len(TEXT_GROUPS))}
        for _, s, k in waits:
            part = (image, text)[s]
            with jax.named_scope(f"arrive_{'it'[s]}{k:02d}"):
                part.arrive(k)
            missing[(s, group_of[s][part.pos[part.g.neg(part.out_route[k][0])]])].discard(k)
            ready = {(h, g) for h, g in todo if not missing[(0, h)] and not missing[(1, g)]}
            todo -= ready
            for hs, gs in rectangles(ready):
                with jax.named_scope(f"pow{hs[0]}{gs[0]}"):
                    powers(hs, gs)

        with jax.named_scope("sums_out"):
            for s, part, sums in ((1, text, col_sums), (0, image, row_sums)):
                for g, row in enumerate(sums):
                    row = row if s else jnp.sum(jnp.transpose(row), axis=0, keepdims=True)
                    for k in range(sizes[s][g]):
                        part.keep_sum(first[s][g] + k, row[:, k * rows : (k + 1) * rows])
                part.start_sums()

        def inverse(part, totals, lines):
            totals[...] = 1.0 / part.total()
            for k, slot in enumerate(part.g.slots):
                lines[:, k * rows : (k + 1) * rows] = totals[pl.ds(part.g.index(slot), 1), 0:rows]

        with jax.named_scope("sums_in"):
            inverse(image, row_tot, row_all)
            row_inv = row_all[...]
            row_inv_up = upright(row_inv)
            inverse(text, col_tot, col_all)
            col_inv = col_all[...]

        def scale(start, end):
            values = power[:, start:end] * (row_inv_up + col_inv[:, start:end])
            if start == 0:
                ids = [lax.broadcasted_iota(jnp.int32, values.shape, d) for d in (0, 1)]
                values = values - jnp.where((ids[0] == ids[1]) & (ids[0] < rows), 2.0, 0.0)
            pull[:, start:end] = values.astype(BF16)

        image.wait_sends(0)
        text.wait_sends(0)
        scaled = pull.shape[1]
        for s, first_slot, end_slot in BACK_ORDER:
            start, end = first_slot * rows, end_slot * rows
            part, own, out = ((image, image_own, image_out), (text, text_own, text_out))[s]
            with jax.named_scope(f"g{'it'[s]}{first_slot}"):
                if scaled > s * start:
                    scale(s * start, scaled)
                    scaled = s * start
                if s == 0:
                    grad = jnp.dot(pull[start:end, :], texts[...], preferred_element_type=F32)
                else:
                    grad = lax.dot_general(pull[:, start:end], images[...], TN, preferred_element_type=F32)
                own[start:end, :] = grad
                out[start:end, :] = grad.astype(BF16)
                part.send_ready(part.g.slots[first_slot:end_slot])
        image_loss[...] = -jnp.log(row_inv[:, 0:rows]) - matched
        text_loss[...] = -jnp.log(col_inv[:, 0:rows]) - matched
        for _, s, k in sorted((t, s, k) for s, part in enumerate((image, text)) for t, k in part.stops()):
            part = (image, text)[s]
            with jax.named_scope(f"pass_{'it'[s]}{k:02d}"):
                part.pass_on(k)
        image_grad[...] = image_own[0:rows, :]
        text_grad[...] = text_own[0:rows, :]
        with jax.named_scope("out"):
            for _, s, k in sorted((t, s, k) for s, part in enumerate((image, text)) for t, k in part.home_pools()):
                (image, text)[s].add_home(k, (image_grad, text_grad)[s])
        with jax.named_scope("wait_sends"):
            for part in (image, text):
                part.wait_sends(0)
                part.wait_sends(1)

    if len(PLANS) == 1:
        run(PLANS[0])
    else:
        for k, plan in enumerate(PLANS):
            pl.when(unit == k)(functools.partial(run, plan))


def place(*refs):
    sem = refs[-1]
    copies = [
        pltpu.make_async_copy(refs[i], refs[i + 4], sem.at[i]) for i in (2, 3, 0, 1)
    ]
    for copy in copies:
        copy.start()
    for copy in copies:
        copy.wait()


def solution(mesh):
    side = mesh.shape["lane"]

    def body(image_rows, text_rows):
        rows, width = image_rows.shape
        nz, npl = mesh.shape["block"] // side, side * side
        images_n, texts_n = nz * rows, npl * rows
        routes = [len(route[0]) for route in PLANS[0]]
        semaphores = (RECV_SEMS[0], RECV_SEMS[1])
        scratch = [
            pltpu.VMEM((rows, width), BF16),
            pltpu.VMEM((rows, width), BF16),
            pltpu.VMEM((images_n, width), BF16),
            pltpu.VMEM((texts_n, width), BF16),
            pltpu.VMEM((images_n, texts_n), F32),
            pltpu.VMEM((images_n, texts_n), BF16),
            pltpu.VMEM((nz, 128), F32),
            pltpu.VMEM((nz - 1, nz, 128), F32),
            pltpu.VMEM((npl, 128), F32),
            pltpu.VMEM((npl - 1, npl, 128), F32),
            pltpu.VMEM((nz, 128), F32),
            pltpu.VMEM((npl, 128), F32),
            pltpu.VMEM((1, images_n), F32),
            pltpu.VMEM((1, texts_n), F32),
            pltpu.VMEM((images_n, width), F32),
            pltpu.VMEM((texts_n, width), F32),
            pltpu.VMEM((images_n, width), BF16),
            pltpu.VMEM((texts_n, width), BF16),
            pltpu.VMEM((routes[0], rows // PIECES, width), BF16),
            pltpu.VMEM((routes[1], rows // PIECES, width), BF16),
        ]
        scratch.append(pltpu.SemaphoreType.REGULAR)
        for count in semaphores:
            scratch += [pltpu.SemaphoreType.DMA((n,)) for n in (2, count, 1)]
        results = pl.pallas_call(
            functools.partial(kernel, side),
            out_shape=(
                jax.ShapeDtypeStruct((1, rows), F32),
                jax.ShapeDtypeStruct((1, rows), F32),
                jax.ShapeDtypeStruct((rows, width), F32),
                jax.ShapeDtypeStruct((rows, width), F32),
            ),
            in_specs=[pl.BlockSpec(memory_space=pltpu.HBM)] * 2,
            out_specs=[pl.BlockSpec(memory_space=pltpu.VMEM)] * 4,
            scratch_shapes=scratch,
            compiler_params=pltpu.CompilerParams(
                collective_id=0, has_side_effects=True, vmem_limit_bytes=40 * 2**20
            ),
        )(*(pltpu.with_memory_space_constraint(x, pltpu.HBM) for x in (image_rows, text_rows)))
        image_loss, text_loss, image_grad, text_grad = pl.pallas_call(
            place,
            out_shape=tuple(jax.ShapeDtypeStruct(r.shape, r.dtype) for r in results),
            in_specs=[pl.BlockSpec(memory_space=pltpu.VMEM)] * 4,
            out_specs=[pl.BlockSpec(memory_space=pl.ANY)] * 4,
            scratch_shapes=[pltpu.SemaphoreType.DMA((4,))],
            compiler_params=pltpu.CompilerParams(vmem_limit_bytes=4 * rows * width * 8),
        )(*results)
        return (image_loss.reshape(rows), text_loss.reshape(rows), image_grad, text_grad)

    rows_spec = P(("unit", "block", "lane"), None)
    flat_spec = P(("unit", "block", "lane"))
    return jax.shard_map(
        body,
        mesh=mesh,
        in_specs=(rows_spec, rows_spec),
        out_specs=(flat_spec, flat_spec, rows_spec, rows_spec),
        check_vma=False,
    )
```

profile of v0, /device:TPU:2, one launch (start us, length us, event | category | flops | bytes accessed | tf_op | source)
XLA Modules:
  0.0 37.0 jit_solution(2758884695874828520)
XLA Ops:
  0.6 35.7 %shard_map.57 = (f32[1,64]{1,0:T(1,128)S(1)}, f32[1,64]{1,0:T(1,128)S(1)}, f32[64,512]{1,0:T(8,128)S(1)}, f32[64,512]{1,0:T(8,128)S(1)}) custom-call(bf16[64,512]{1,0:T(8,128)(2,1)} %image_hbm.1, bf16[64,512]{1,0:T(8,128)(2,1)} %text_hbm.1), custom_call_target="tpu_custom_call" | custom-call | tf_op jit(solution)/shard_map/pallas_call | solution.py:505
  36.3 0.7 %shard_map.58 = (f32[1,64]{1,0:T(1,128)}, f32[1,64]{1,0:T(1,128)}, f32[64,512]{1,0:T(8,128)}, f32[64,512]{1,0:T(8,128)}) custom-call(f32[1,64]{1,0:T(1,128)S(1)} %get-tuple-element.12.refs_0_, f32[1,64]{1,0:T(1,128)S(1)} %get-tuple-element.13.refs_1_, f32[64,512]{1,0:T(8,128)S(1)} %get-tuple-element.14.refs_2_, f32[64,512]{1,0:T(8,128)S(1)} %get-tuple-element.15.refs_3_), custom_call_target="tpu_custom_call" | custom-call | tf_op jit(solution)/shard_map/pallas_call | solution.py:520
where the time goes:
time: 37.4 us; the launch traced here: 37 us
  Pallas kernels  36.4 us (97%)
  between operations  0.64 us (2%)
    pallas_call x1, Pallas kernels, body(): pl.pallas_call(functools.partial(kernel, side), out_shape=(jax.ShapeDtype...  35.7 us

commit v1 on v0

--- a/solution.py
+++ b/solution.py
@@ -12,7 +12,7 @@
 LOG2E = 1.4426950408889634
 F32, BF16 = jnp.float32, jnp.bfloat16
 PIECES = 2
-RECV_SEMS = (12, 22)
+RECV_SEMS = (10, 18)
 BACK_ORDER = [(1, 12, 16), (0, 4, 8), (1, 8, 12), (0, 0, 4), (1, 4, 8), (1, 0, 4)]
 IMAGE_GROUPS, TEXT_GROUPS = (4, 4), (4, 4, 8)
 
@@ -347,14 +347,14 @@
         text.start_gather(1)
         image.start_gather(1)
 
-        pair = 12.0 * lax.dot_general(images[0:rows, :], texts[0:rows, :], NT, preferred_element_type=F32)
-        eye = lax.broadcasted_iota(jnp.int32, (rows, rows), 0) == lax.broadcasted_iota(jnp.int32, (rows, rows), 1)
-        matched = jnp.sum(jnp.where(eye, pair, 0.0), axis=0, keepdims=True)
-
         with jax.named_scope("around"):
             pl.semaphore_wait(around, len(image.next_to()) + len(text.next_to()))
         text.start_gather(2)
         image.start_gather(2)
+
+        pair = 12.0 * lax.dot_general(images[0:rows, :], texts[0:rows, :], NT, preferred_element_type=F32)
+        eye = lax.broadcasted_iota(jnp.int32, (rows, rows), 0) == lax.broadcasted_iota(jnp.int32, (rows, rows), 1)
+        matched = jnp.sum(jnp.where(eye, pair, 0.0), axis=0, keepdims=True)
 
         row_sums, col_sums = [0.0] * len(IMAGE_GROUPS), [0.0] * len(TEXT_GROUPS)
 
@@ -370,6 +370,12 @@
                     end = start + sizes[s][g] * rows
                     sums[g] += jnp.sum(p[:, start:end], axis=0, keepdims=True) if s else lanes[start:end]
                     start = end
+
+        def keep_sums(s, g):
+            part, row = (image, text)[s], (row_sums, col_sums)[s][g]
+            row = row if s else jnp.sum(jnp.transpose(row), axis=0, keepdims=True)
+            for k in range(sizes[s][g]):
+                part.keep_sum(first[s][g] + k, row[:, k * rows : (k + 1) * rows])
 
         waits = sorted(
             (t, s, k) for s, part in enumerate((image, text)) for k, (_, _, _, t) in enumerate(part.out_route)
@@ -389,14 +395,14 @@
             for hs, gs in rectangles(ready):
                 with jax.named_scope(f"pow{hs[0]}{gs[0]}"):
                     powers(hs, gs)
+            for g in sorted({g for _, g in ready} - {g for _, g in todo}):
+                keep_sums(1, g)
 
         with jax.named_scope("sums_out"):
-            for s, part, sums in ((1, text, col_sums), (0, image, row_sums)):
-                for g, row in enumerate(sums):
-                    row = row if s else jnp.sum(jnp.transpose(row), axis=0, keepdims=True)
-                    for k in range(sizes[s][g]):
-                        part.keep_sum(first[s][g] + k, row[:, k * rows : (k + 1) * rows])
-                part.start_sums()
+            text.start_sums()
+            for h in range(len(IMAGE_GROUPS)):
+                keep_sums(0, h)
+            image.start_sums()
 
         def inverse(part, totals, lines):
             totals[...] = 1.0 / part.total()

time: 37.4 us -> 37.4 us (level)
  no operation moved by 1% of the time
where the time goes in v1:
time: 37.4 us; the launch traced here: 36.9 us
  Pallas kernels  36.2 us (97%)
  between operations  0.64 us (2%)
    pallas_call x1, Pallas kernels, body(): pl.pallas_call(functools.partial(kernel, side), out_shape=(jax.ShapeDtype...  35.5 us

profile of v1, /device:TPU:2, one launch (start us, length us, event | category | flops | bytes accessed | tf_op | source)
XLA Modules:
  0.0 36.9 jit_solution(13273294439296494032)
XLA Ops:
  0.6 35.5 %shard_map.57 = (f32[1,64]{1,0:T(1,128)S(1)}, f32[1,64]{1,0:T(1,128)S(1)}, f32[64,512]{1,0:T(8,128)S(1)}, f32[64,512]{1,0:T(8,128)S(1)}) custom-call(bf16[64,512]{1,0:T(8,128)(2,1)} %image_hbm.1, bf16[64,512]{1,0:T(8,128)(2,1)} %text_hbm.1), custom_call_target="tpu_custom_call" | custom-call | tf_op jit(solution)/shard_map/pallas_call | solution.py:511
  36.1 0.7 %shard_map.58 = (f32[1,64]{1,0:T(1,128)}, f32[1,64]{1,0:T(1,128)}, f32[64,512]{1,0:T(8,128)}, f32[64,512]{1,0:T(8,128)}) custom-call(f32[1,64]{1,0:T(1,128)S(1)} %get-tuple-element.12.refs_0_, f32[1,64]{1,0:T(1,128)S(1)} %get-tuple-element.13.refs_1_, f32[64,512]{1,0:T(8,128)S(1)} %get-tuple-element.14.refs_2_, f32[64,512]{1,0:T(8,128)S(1)} %get-tuple-element.15.refs_3_), custom_call_target="tpu_custom_call" | custom-call | tf_op jit(solution)/shard_map/pallas_call | solution.py:526

commit v2 on v1

--- a/solution.py
+++ b/solution.py
@@ -349,8 +349,8 @@
 
         with jax.named_scope("around"):
             pl.semaphore_wait(around, len(image.next_to()) + len(text.next_to()))
+        image.start_gather(2)
         text.start_gather(2)
-        image.start_gather(2)
 
         pair = 12.0 * lax.dot_general(images[0:rows, :], texts[0:rows, :], NT, preferred_element_type=F32)
         eye = lax.broadcasted_iota(jnp.int32, (rows, rows), 0) == lax.broadcasted_iota(jnp.int32, (rows, rows), 1)

time: 37.4 us -> 37.4 us (level)
  no operation moved by 1% of the time
where the time goes in v2:
time: 37.4 us; the launch traced here: 36.9 us
  Pallas kernels  36.2 us (97%)
  between operations  0.64 us (2%)
    pallas_call x1, Pallas kernels, body(): pl.pallas_call(functools.partial(kernel, side), out_shape=(jax.ShapeDtype...  35.5 us

profile of v2, /device:TPU:2, one launch (start us, length us, event | category | flops | bytes accessed | tf_op | source)
XLA Modules:
  0.0 36.9 jit_solution(16488916809488396232)
XLA Ops:
  0.6 35.5 %shard_map.57 = (f32[1,64]{1,0:T(1,128)S(1)}, f32[1,64]{1,0:T(1,128)S(1)}, f32[64,512]{1,0:T(8,128)S(1)}, f32[64,512]{1,0:T(8,128)S(1)}) custom-call(bf16[64,512]{1,0:T(8,128)(2,1)} %image_hbm.1, bf16[64,512]{1,0:T(8,128)(2,1)} %text_hbm.1), custom_call_target="tpu_custom_call" | custom-call | tf_op jit(solution)/shard_map/pallas_call | solution.py:511
  36.1 0.7 %shard_map.58 = (f32[1,64]{1,0:T(1,128)}, f32[1,64]{1,0:T(1,128)}, f32[64,512]{1,0:T(8,128)}, f32[64,512]{1,0:T(8,128)}) custom-call(f32[1,64]{1,0:T(1,128)S(1)} %get-tuple-element.12.refs_0_, f32[1,64]{1,0:T(1,128)S(1)} %get-tuple-element.13.refs_1_, f32[64,512]{1,0:T(8,128)S(1)} %get-tuple-element.14.refs_2_, f32[64,512]{1,0:T(8,128)S(1)} %get-tuple-element.15.refs_3_), custom_call_target="tpu_custom_call" | custom-call | tf_op jit(solution)/shard_map/pallas_call | solution.py:526
